TPU v7x, 256 devices: a whole 4x4x8 slice. The times are simulated.
256 devices in a mesh: energy: 16 (over x, z_lo, core), kpt: 4 (over z_hi), layer: 4 (over y).
Axes of the slice: x: 4, y: 4, z: 8 (z_hi: 4, z_lo: 2; z = z_hi * 2 + z_lo), core: 2. Of those that a mesh axis runs over, the one named last changes fastest.
Arguments:
- energies: float32 [64], P(('energy', 'layer')), may hold values from -1.5 to 1.5
- momenta: float32 [4], P('kpt'), may hold values from 0 to 1
- energy_level: int32 [64], P(('energy', 'layer')), may hold values from 0 to 7
- momentum_level: int32 [4], P('kpt'), may hold values from 0 to 7
- energy_table: float32 [8], replicated, may hold values from 0.25 to 4
- momentum_table: float32 [8], replicated, may hold values from 0.25 to 4
- onsite: float32 [5, 256, 256], replicated, may hold values from -1 to 1, as said below
- broad: float32 [5, 256], replicated, may hold values from 1 to 4
- kdiag: float32 [5, 256], replicated, may hold values from 0.2 to 2
- fermi: float32 [5], replicated, may hold values from -1 to 1
- couplings: float32 [3, 256, 256], replicated, may hold values from -0.0624 to 0.0624
- bond_kind: int32 [4], replicated, may hold values from 0 to 2
Outputs:
- density: float32 [4, 2, 256, 256], P('layer', None, 'energy')
- current: float32 [4, 2, 256, 256], P('layer', None, 'energy')
Inputs may be any that keep to these rules, and one draw needn't show every extreme that they name: Each block of onsite is symmetric.
All inputs are finite; a program needn't handle non-finite values.
Results may differ from a plain program's by a relative error of at most 0.0001.
Values sent between devices are 32-bit elements; how exact they have to be, the bound alone decides.
A program may use at most 64 MiB of HBM per device.

v0:
```python
import jax
import jax.numpy as jnp
from jax import lax
from jax.experimental import pallas as pl
from jax.experimental.pallas import tpu as pltpu
from jax.sharding import PartitionSpec as P

bf16 = jnp.bfloat16
f32 = jnp.float32
B = 256


def dot(a, b, tb=False):
    return lax.dot_general(
        a, b, (((1,), (1 if tb else 0,)), ((), ())), preferred_element_type=f32
    )


def split(x):
    high = x.astype(bf16)
    return high, (x - high.astype(f32)).astype(bf16)


def dot3(left, right, tb=False):
    return (
        dot(left[0], right[0], tb) + dot(left[0], right[1], tb) + dot(left[1], right[0], tb)
    )


def put(pair, at, x):
    high, low = split(x)
    pair[0][at] = high
    pair[1][at] = low


def put_left(pair, lead, row, re, im, conj):
    for ref, r, i in zip(pair, split(re), split(im)):
        top = lead + (pl.ds(row, B),)
        low = lead + (pl.ds(row + B, B),)
        a, b = pl.ds(0, B), pl.ds(B, B)
        ref[top + (a,)] = r
        ref[low + (a,)] = i
        ref[top + (b,)] = i if conj else -i
        ref[low + (b,)] = -r if conj else r


def sweeps(
    e_ref, k_ref, el_ref, ml_ref, et_ref, mt_ref, fermi_ref, bk_ref,
    onsite, broad, kdiag, couplings, density, current,
    gw_h, gw_l, pr_h, pr_l, x_h, x_l, s_h, s_l, a_h, a_l, v_h, v_l, vt_h, vt_l, gf, wf,
    blocks, from_core, to_plane, from_plane, to_line, from_line, to_owner, at_owner, owned,
    core_sems, plane_sems, line_sems, owner_sems,
):
    layers = onsite.shape[0] - 1
    gw, pr, xs, ss, aa, vv, vt = (
        (gw_h, gw_l), (pr_h, pr_l), (x_h, x_l), (s_h, s_l), (a_h, a_l), (v_h, v_l), (vt_h, vt_l)
    )
    energy = e_ref[0]
    moment = k_ref[0]
    weight = et_ref[el_ref[0]] * mt_ref[ml_ref[0]] * (1.0 / 256)
    me_e, me_k, me_l = lax.axis_index("energy"), lax.axis_index("kpt"), lax.axis_index("layer")
    me_x, me_z, me_c = lax.div(me_e, 4), lax.rem(lax.div(me_e, 2), 2), lax.rem(me_e, 2)

    def device(x, z, c, k, y):
        return ((x * 2 + z) * 2 + c, k, y)

    def core_peer():
        return device(me_x, me_z, 1 - me_c, me_k, me_l)

    def plane_peer(step):
        return lax.rem(me_x + step // 4, 4), lax.rem(me_l + step % 4, 4)

    def line_peer(step):
        return lax.rem(me_z + step // 4, 2), lax.rem(me_k + step % 4, 4)

    def owner_peer(step):
        return lax.rem(me_k + step // 4, 4), lax.rem(me_l + step % 4, 4)

    def plane_device(step):
        x, y = plane_peer(step)
        return device(x, me_z, me_c, me_k, y)

    def line_device(step):
        z, k = line_peer(step)
        return device(me_x, z, me_c, k, me_l)

    def owner_device(step):
        k, y = owner_peer(step)
        return device(me_x, me_z, me_c, k, y)

    barrier = pltpu.get_barrier_semaphore()
    peers = [core_peer()] + [plane_device(s) for s in range(1, 16)]
    peers += [line_device(s) for s in range(1, 8)] + [owner_device(s) for s in range(1, 16)]
    for peer in peers:
        pl.semaphore_signal(barrier, inc=1, device_id=peer, device_id_type=pl.DeviceIdType.MESH)

    def send(src, dst, sems, peer):
        pltpu.make_async_remote_copy(
            src_ref=src, dst_ref=dst, send_sem=sems[0], recv_sem=sems[1],
            device_id=peer, device_id_type=pl.DeviceIdType.MESH,
        ).start()

    def wait(like, sem):
        pltpu.make_async_copy(like, like, sem).wait()

    def core_start(i):
        send(blocks.at[i, :, :, :, 1 - me_c], from_core.at[i],
             (core_sems.at[0, i], core_sems.at[1, i]), core_peer())

    def core_finish(i):
        wait(from_core.at[i], core_sems.at[1, i])
        to_plane[i] = blocks[i, :, :, :, me_c] + from_core[i]

    def plane_start(i):
        for step in range(1, 16):
            x, y = plane_peer(step)
            send(to_plane.at[i, y, x], from_plane.at[i, step - 1],
                 (plane_sems.at[0, i], plane_sems.at[1, i]), plane_device(step))

    def plane_finish(i):
        wait(from_plane.at[i], plane_sems.at[1, i])
        total = to_plane[i, me_l, me_x]
        for step in range(1, 16):
            total = total + from_plane[i, step - 1]
        for z in range(2):
            for k in range(4):
                row, col = 8 * (k // 2), 128 * (k % 2)
                to_line[i, z, k] = total[z, row : row + 8, col : col + 128]

    def line_start(i):
        for step in range(1, 8):
            z, k = line_peer(step)
            send(to_line.at[i, z, k], from_line.at[i, step - 1],
                 (line_sems.at[0, i], line_sems.at[1, i]), line_device(step))

    def line_finish(i):
        wait(from_line.at[i], line_sems.at[1, i])
        total = to_line[i, me_z, me_k]
        for step in range(1, 8):
            total = total + from_line[i, step - 1]
        to_owner[i] = total

    def owner_exchange():
        for step in range(1, 16):
            k, y = owner_peer(step)
            send(to_owner.at[y], at_owner.at[step - 1],
                 (owner_sems.at[0], owner_sems.at[1]), owner_device(step))
        wait(at_owner, owner_sems.at[1])
        owned[me_l, me_k] = to_owner[me_l]
        for step in range(1, 16):
            k = lax.rem(me_k + 4 - step // 4, 4)
            y = lax.rem(me_l + 4 - step % 4, 4)
            owned[y, k] = at_owner[step - 1]
        for m in range(2):
            for k in range(4):
                at = (0, m, pl.ds(8 * (k // 2), 8), pl.ds(128 * (k % 2), 128))
                density[at] = owned[m, k]
                current[at] = owned[2 + m, k]

    eye = lax.broadcasted_iota(jnp.int32, (B, B), 0) == lax.broadcasted_iota(jnp.int32, (B, B), 1)
    get = lambda pair, *at: (pair[0][at], pair[1][at])

    def forward(i, inner):
        br = broad[i]
        gamma = br * jax.nn.sigmoid(jnp.full((1, B), (fermi_ref[i] - energy) / 0.25, f32))
        if inner:
            kind = bk_ref[i - 1]
            v = jnp.where(kind == 0, couplings[0], jnp.where(kind == 1, couplings[1], couplings[2]))
            put(vv, (slice(None),), v)
            put(vt, (slice(None),), v.T)
            p = dot3(get(gw), get(vv))
            put_left(pr, (i - 1,), 0, p[0:B], p[B : 2 * B], False)
            put_left(pr, (i - 1,), 2 * B, p[2 * B : 3 * B], p[3 * B :], True)
            left = get(vt)
            part = lambda j: dot3(left, get(pr, i - 1, pl.ds(j * B, B), pl.ds(0, B)))
            m_re = -onsite[i] - part(0)
            m_im = -part(1)
            s_re = part(2) + jnp.where(eye, gamma, 0.0)
            s_im = part(3)
        else:
            m_re = -onsite[i]
            s_re = jnp.where(eye, gamma, 0.0)
        shift = energy - moment * kdiag[i]
        dr = jnp.where(eye, m_re + shift, 0.0)
        dr_row, dr_col = jnp.sum(dr, 0, keepdims=True), jnp.sum(dr, 1, keepdims=True)
        half = 0.5 * br
        di = jnp.where(eye, (m_im + half) if inner else half, 0.0)
        di_row, di_col = jnp.sum(di, 0, keepdims=True), jnp.sum(di, 1, keepdims=True)
        n_row = 1.0 / (dr_row * dr_row + di_row * di_row)
        n_col = 1.0 / (dr_col * dr_col + di_col * di_col)
        rr, ri = dr_row * n_row, -di_row * n_row
        cr, ci = dr_col * n_col, -di_col * n_col
        off = jnp.where(eye, 0.0, m_re)
        if inner:
            off_im = jnp.where(eye, 0.0, m_im)
            a_re = cr * off - ci * off_im
            a_im = cr * off_im + ci * off
        else:
            a_re, a_im = cr * off, ci * off
        put_left(xs, (), 0, a_re, a_im, False)
        sq = dot3(get(xs, pl.ds(0, 2 * B), slice(None)), get(xs, pl.ds(0, 2 * B), pl.ds(0, B)))
        u_re, u_im = sq[0:B], sq[B:]
        put_left(aa, (), 0, u_re, u_im, False)
        cube = dot3(get(aa), get(xs, pl.ds(0, 2 * B), pl.ds(0, B)))
        t_re = jnp.where(eye, 1.0, 0.0) - a_re + (u_re - cube[0:B])
        t_im = (u_im - cube[B:]) - a_im
        g_re = t_re * rr - t_im * ri
        g_im = t_re * ri + t_im * rr
        gf[i, pl.ds(0, B)] = g_re
        gf[i, pl.ds(B, B)] = g_im
        put(gw, (pl.ds(0, B),), g_re)
        put(gw, (pl.ds(B, B),), g_im)
        if inner:
            put_left(aa, (), 0, g_re, g_im, False)
            put(ss, (pl.ds(0, B),), s_re)
            put(ss, (pl.ds(B, B),), s_im)
            t = dot3(get(aa), get(ss))
            t_re, t_im = t[0:B], t[B:]
        else:
            t_re, t_im = g_re * gamma, g_im * gamma
        put_left(xs, (), 0, t_re, t_im, True)
        w = dot3(get(xs, pl.ds(0, 2 * B), slice(None)), get(gw, pl.ds(0, 2 * B)))
        wf[i] = w
        put(gw, (pl.ds(2 * B, 2 * B),), w)

    forward(0, False)

    def forward_step(i, carry):
        forward(i, True)
        return carry

    lax.fori_loop(1, layers + 1, forward_step, 0)
    pl.semaphore_wait(barrier, len(peers))

    def report(i, m, x):
        blocks[i, m] = (weight * x).reshape(blocks.shape[2:])

    def reach(i, pw, zh, row):
        cur = pw + zh
        report(i, 2, cur[0:B])
        report(i, 3, cur[B:])
        mid = 0.5 * pw + zh
        put_left(xs, (), row, mid[0:B], mid[B:], False)

    def lesser(i, spread):
        h_re, h_im = spread[0:B], spread[B:]
        w_re = wf[i, pl.ds(0, B)] + (h_re + h_re.T)
        w_im = wf[i, pl.ds(B, B)] + (h_im - h_im.T)
        report(i, 0, w_re)
        report(i, 1, w_im)
        return w_re, w_im

    def backward_step(step, carry):
        i = layers - 1 - step
        qz = dot3(get(pr, i), get(gw, pl.ds(0, 2 * B)))
        pw = dot3(get(pr, i, pl.ds(0, 2 * B)), get(gw, pl.ds(2 * B, 2 * B)))
        put_left(xs, (), 0, qz[0:B], qz[B : 2 * B], True)
        reach(i, pw, qz[2 * B :], 2 * B)

        @pl.when(step >= 1)
        def _():
            core_finish(i + 1)
            plane_start(i + 1)

        spread = dot3(get(xs), get(pr, i, pl.ds(0, B)), True)
        put(gw, (pl.ds(0, 2 * B),), gf[i] + spread[0 : 2 * B])
        w_re, w_im = lesser(i, spread[2 * B :])
        put(gw, (pl.ds(2 * B, B),), w_re)
        put(gw, (pl.ds(3 * B, B),), w_im)

        core_start(i)

        @pl.when(step >= 2)
        def _():
            plane_finish(i + 2)
            line_start(i + 2)

        return carry

    lax.fori_loop(0, layers - 1, backward_step, 0)
    zh = dot3(get(pr, 0, pl.ds(2 * B, 2 * B)), get(gw, pl.ds(0, 2 * B)))
    pw = dot3(get(pr, 0, pl.ds(0, 2 * B)), get(gw, pl.ds(2 * B, 2 * B)))
    reach(0, pw, zh, 0)
    core_finish(1)
    plane_start(1)
    spread = dot3(get(xs, pl.ds(0, 2 * B)), get(pr, 0, pl.ds(0, B)), True)
    lesser(0, spread)
    core_start(0)
    plane_finish(2)
    line_start(2)
    core_finish(0)
    plane_start(0)
    plane_finish(1)
    line_start(1)
    plane_finish(0)
    line_start(0)
    for i in (3, 2, 1, 0):
        line_finish(i)
    owner_exchange()
    for i in range(layers):
        wait(from_core.at[i], core_sems.at[0, i])
        wait(from_plane.at[i], plane_sems.at[0, i])
        wait(from_line.at[i], line_sems.at[0, i])
    wait(at_owner, owner_sems.at[0])


def scratch(layers):
    pair = lambda *s: [pltpu.VMEM(s, bf16), pltpu.VMEM(s, bf16)]
    full = lambda *s: pltpu.VMEM(s, f32)
    return (
        pair(4 * B, B) + pair(layers, 4 * B, 2 * B) + pair(4 * B, 2 * B) + pair(2 * B, B)
        + pair(2 * B, 2 * B) + pair(B, B) + pair(B, B)
        + [full(layers + 1, 2 * B, B)] * 2
        + [
            full(layers, 4, 4, 2, 2, 16, B),
            full(layers, 4, 4, 2, 16, B),
            full(layers, 4, 4, 2, 16, B),
            full(layers, 15, 2, 16, B),
            full(layers, 2, 4, 8, 128),
            full(layers, 7, 8, 128),
            full(layers, 8, 128),
            full(15, 8, 128),
            full(4, 4, 8, 128),
            pltpu.SemaphoreType.DMA((2, layers)),
            pltpu.SemaphoreType.DMA((2, layers)),
            pltpu.SemaphoreType.DMA((2, layers)),
            pltpu.SemaphoreType.DMA((2,)),
        ]
    )


def per_device(
    energies, momenta, energy_level, momentum_level, energy_table, momentum_table,
    onsite, broad, kdiag, fermi, couplings, bond_kind,
):
    smem = pl.BlockSpec(memory_space=pltpu.SMEM)
    vmem = pl.BlockSpec(memory_space=pltpu.VMEM)
    layers = onsite.shape[0] - 1
    result = jax.ShapeDtypeStruct((1, 2, 16, B), f32)
    return pl.pallas_call(
        sweeps,
        out_shape=(result, result),
        in_specs=[smem] * 8 + [vmem] * 4,
        out_specs=(vmem, vmem),
        scratch_shapes=scratch(layers),
        compiler_params=pltpu.CompilerParams(
            vmem_limit_bytes=62 << 20, collective_id=0, has_side_effects=True
        ),
        name="sweeps",
    )(
        energies, momenta, energy_level, momentum_level, energy_table, momentum_table,
        fermi, bond_kind, onsite, broad[:, None, :], kdiag[:, None, :], couplings,
    )


def solution(mesh):
    rep = P()
    both = P(("energy", "layer"))
    return jax.shard_map(
        per_device,
        mesh=mesh,
        in_specs=(both, P("kpt"), both, P("kpt"), rep, rep, rep, rep, rep, rep, rep, rep),
        out_specs=(P("layer", None, "energy", None), P("layer", None, "energy", None)),
        check_vma=False,
    )
```

profile of v0, /device:TPU:8, one launch (start us, length us, event | category | flops | bytes accessed | tf_op | source)
XLA Modules:
  0.0 81.7 jit_solution(6018556445182171157)
XLA Ops:
  3.2 1.3 %broadcast_in_dim.6.broad = f32[5,1,256]{2,1,0:T(1,128)} reshape(f32[5,256]{1,0:T(8,128)} %param.19) | data formatting | bytes 10240 | tf_op jit(solution)/shard_map/broadcast_in_dim | solution.py:352
  4.5 1.3 %broadcast_in_dim.7.kdiag = f32[5,1,256]{2,1,0:T(1,128)} reshape(f32[5,256]{1,0:T(8,128)} %param.20) | data formatting | bytes 10240 | tf_op jit(solution)/shard_map/broadcast_in_dim | solution.py:352
  5.8 73.2 %sweeps.1 = (f32[1,2,16,256]{3,2,1,0:T(8,128)}, f32[1,2,16,256]{3,2,1,0:T(8,128)}) custom-call(f32[1]{0:T(128)S(6)} %copy.16.e_ref, f32[1]{0:T(128)S(6)} %copy.17.k_ref, s32[1]{0:T(128)S(6)} %copy.18.el_ref, s32[1]{0:T(128)S(6)} %copy.19.ml_ref, f32[8]{0:T(128)} %et_ref.1, f32[8]{0:T(128)} %mt_ref.1, f32[5]{0:T(128)} %fermi_ref.1, s32[4]{0:T(128)} %bk_ref.1, ...), custom_call_target="tpu_custom_call" | custom-call | tf_op jit(solution)/shard_map/sweeps/pallas_call | solution.py:340
  79.0 1.4 %copy.20 = f32[1,2,16,256]{3,2,1,0:T(8,128)} copy(f32[1,2,16,256]{3,2,1,0:T(8,128)} %get-tuple-element.4) | data formatting | bytes 65536
  80.4 1.4 %copy.21 = f32[1,2,16,256]{3,2,1,0:T(8,128)} copy(f32[1,2,16,256]{3,2,1,0:T(8,128)} %get-tuple-element.5) | data formatting | bytes 65536
where the time goes:
time: 82.1 us; the launch traced here: 81.7 us
  Pallas kernels  73.2 us (89%)
  local copies, waits for them, and re-layouts  5.34 us (7%)
  between operations  3.22 us (4%)
    pallas_call x1, Pallas kernels, per_device(): pl.pallas_call(sweeps, out_shape=(result, result), in_specs=[smem] * 8 +...  73.2 us
    unnamed x2, local copies, waits for them, and re-layouts  2.75 us

commit v1 on v0

v1 whole, which is shorter than its diff:
```python
import jax
import jax.numpy as jnp
from jax import lax
from jax.experimental import pallas as pl
from jax.experimental.pallas import tpu as pltpu
from jax.sharding import PartitionSpec as P

bf16 = jnp.bfloat16
f32 = jnp.float32
B = 256
CH = 32


def dot(a, b, tb=False):
    return lax.dot_general(
        a, b, (((1,), (1 if tb else 0,)), ((), ())), preferred_element_type=f32
    )


def split(x):
    high = x.astype(bf16)
    return high, (x - high.astype(f32)).astype(bf16)


def dot3(left, right, tb=False):
    return (
        dot(left[0], right[0], tb) + dot(left[0], right[1], tb) + dot(left[1], right[0], tb)
    )


def get(pair, *at):
    return pair[0][at], pair[1][at]


def put(pair, at, x):
    pair[0][at], pair[1][at] = split(x)


def put_left(pair, lead, row, rows, re, im, conj):
    for ref, r, i in zip(pair, split(re), split(im)):
        top, low = lead + (pl.ds(row, rows),), lead + (pl.ds(row + B, rows),)
        a, b = pl.ds(0, B), pl.ds(B, B)
        ref[top + (a,)] = r
        ref[low + (a,)] = i
        ref[top + (b,)] = i if conj else -i
        ref[low + (b,)] = -r if conj else r


def chunks():
    for r in range(0, B, CH):
        yield r, slice(r, r + CH), slice(B + r, B + r + CH)


def sweeps(
    *refs,
):
    scalars, inputs, result = refs[:8], refs[8:12], refs[12]
    held, in_sems, rest = refs[13:17], refs[17], refs[18:]
    copies = [pltpu.make_async_copy(a, b, in_sems.at[n]) for n, (a, b) in enumerate(zip(inputs, held))]
    for copy in copies:
        copy.start()
    sweep_body(copies, result, *scalars, *held, *rest)


def sweep_body(
    copies, result, e_ref, k_ref, el_ref, ml_ref, et_ref, mt_ref, fermi_ref, bk_ref,
    broad, kdiag, couplings, onsite,
    gs_h, gs_l, gl_h, gl_l, ws_h, ws_l, pr_h, pr_l, al_h, al_l, ul_h, ul_l, ss_h, ss_l,
    tl_h, tl_l, ml_h, ml_l, v_h, v_l, vt_h, vt_l, gf, wf, mf, hf,
    blocks, from_core, to_plane, from_first, to_second, from_second, to_line, from_line, to_owner, at_owner, owned,
    core_sems, first_sems, second_sems, line_sems, owner_sems,
):
    layers = onsite.shape[0] - 1
    gs, gl, ws, pr, al, ul, ss, tl, ml, vv, vt = (
        (gs_h, gs_l), (gl_h, gl_l), (ws_h, ws_l), (pr_h, pr_l), (al_h, al_l), (ul_h, ul_l),
        (ss_h, ss_l), (tl_h, tl_l), (ml_h, ml_l), (v_h, v_l), (vt_h, vt_l),
    )
    for copy in copies:
        copy.wait()
    energy = e_ref[0]
    moment = k_ref[0]
    weight = et_ref[el_ref[0]] * mt_ref[ml_ref[0]] * (1.0 / 256)
    me_e, me_k, me_l = lax.axis_index("energy"), lax.axis_index("kpt"), lax.axis_index("layer")
    me_x, me_z, me_c = lax.div(me_e, 4), lax.rem(lax.div(me_e, 2), 2), lax.rem(me_e, 2)

    def device(x, z, c, k, y):
        return ((x * 2 + z) * 2 + c, k, y)

    def core_peer():
        return device(me_x, me_z, 1 - me_c, me_k, me_l)

    def after(at, step):
        return lax.rem(at + step, 4)

    def x_device(step):
        return device(after(me_x, step), me_z, me_c, me_k, me_l)

    def y_device(step):
        return device(me_x, me_z, me_c, me_k, after(me_l, step))

    def line_peer(step):
        return lax.rem(me_z + step // 4, 2), lax.rem(me_k + step % 4, 4)

    def owner_peer(step):
        return lax.rem(me_k + step // 4, 4), lax.rem(me_l + step % 4, 4)

    def line_device(step):
        z, k = line_peer(step)
        return device(me_x, z, me_c, k, me_l)

    def owner_device(step):
        k, y = owner_peer(step)
        return device(me_x, me_z, me_c, k, y)

    barrier = pltpu.get_barrier_semaphore()
    peers = [core_peer()] + [x_device(s) for s in range(1, 4)]
    peers += [line_device(s) for s in range(1, 8)] + [owner_device(s) for s in range(1, 16)]
    for peer in peers:
        pl.semaphore_signal(barrier, inc=1, device_id=peer, device_id_type=pl.DeviceIdType.MESH)

    def send(src, dst, sems, peer):
        pltpu.make_async_remote_copy(
            src_ref=src, dst_ref=dst, send_sem=sems[0], recv_sem=sems[1],
            device_id=peer, device_id_type=pl.DeviceIdType.MESH,
        ).start()

    def wait(like, sem):
        pltpu.make_async_copy(like, like, sem).wait()

    def core_start(i):
        send(blocks.at[i, :, :, :, 1 - me_c], from_core.at[i],
             (core_sems.at[0, i], core_sems.at[1, i]), core_peer())

    def core_finish(i):
        wait(from_core.at[i], core_sems.at[1, i])
        to_plane[i] = blocks[i, :, :, :, me_c] + from_core[i]

    def plane_start(i):
        for step in range(1, 4):
            send(to_plane.at[i, :, after(me_x, step), 0], from_first.at[i, 0, step - 1],
                 (first_sems.at[0, 0, i], first_sems.at[1, 0, i]), x_device(step))
            send(to_plane.at[i, after(me_l, step), :, 1], from_first.at[i, 1, step - 1],
                 (first_sems.at[0, 1, i], first_sems.at[1, 1, i]), y_device(step))

    def plane_turn(i):
        for way in range(2):
            wait(from_first.at[i, way], first_sems.at[1, way, i])
            own = to_plane[i, :, me_x, 0] if way == 0 else to_plane[i, me_l, :, 1]
            to_second[i, way] = own + from_first[i, way, 0] + (
                from_first[i, way, 1] + from_first[i, way, 2]
            )
        for step in range(1, 4):
            send(to_second.at[i, 0, after(me_l, step)], from_second.at[i, 0, step - 1],
                 (second_sems.at[0, 0, i], second_sems.at[1, 0, i]), y_device(step))
            send(to_second.at[i, 1, after(me_x, step)], from_second.at[i, 1, step - 1],
                 (second_sems.at[0, 1, i], second_sems.at[1, 1, i]), x_device(step))

    def plane_finish(i):
        for z in range(2):
            wait(from_second.at[i, z], second_sems.at[1, z, i])
            total = to_second[i, z, me_l if z == 0 else me_x] + from_second[i, z, 0] + (
                from_second[i, z, 1] + from_second[i, z, 2]
            )
            for k in range(4):
                row, col = 8 * (k // 2), 128 * (k % 2)
                to_line[i, z, k] = total[row : row + 8, col : col + 128]

    def line_start(i):
        for step in range(1, 8):
            z, k = line_peer(step)
            send(to_line.at[i, z, k], from_line.at[i, step - 1],
                 (line_sems.at[0, i], line_sems.at[1, i]), line_device(step))

    def line_finish(i):
        wait(from_line.at[i], line_sems.at[1, i])
        total = to_line[i, me_z, me_k]
        for step in range(1, 8):
            total = total + from_line[i, step - 1]
        to_owner[i] = total

    def owner_exchange():
        for step in range(1, 16):
            k, y = owner_peer(step)
            send(to_owner.at[y], at_owner.at[step - 1],
                 (owner_sems.at[0], owner_sems.at[1]), owner_device(step))
        wait(at_owner, owner_sems.at[1])
        owned[me_l, me_k] = to_owner[me_l]
        for step in range(1, 16):
            k = lax.rem(me_k + 4 - step // 4, 4)
            y = lax.rem(me_l + 4 - step % 4, 4)
            owned[y, k] = at_owner[step - 1]
        for m in range(4):
            for k in range(4):
                result[m, pl.ds(8 * (k // 2), 8), pl.ds(128 * (k % 2), 128)] = owned[m, k]

    both, first = pl.ds(0, 2 * B), pl.ds(0, B)

    def diagonal_of(r, lanes):
        at = r % 128 if lanes == 128 else r
        return (
            lax.broadcasted_iota(jnp.int32, (CH, lanes), 0) + at
            == lax.broadcasted_iota(jnp.int32, (CH, lanes), 1)
        )

    def source(i):
        br = broad[pl.ds(i, 1), :]
        return br * jax.nn.sigmoid(jnp.full((1, B), (fermi_ref[i] - energy) / 0.25, f32))

    def inverse_ends(i):
        shift = energy - moment * kdiag[pl.ds(i, 1), :]
        half = 0.5 * broad[pl.ds(i, 1), :]
        rows = []
        cols = {}
        for t in range(2):
            lane = slice(128 * t, 128 * t + 128)
            dr_row = di_row = 0.0
            for r in range(128 * t, 128 * t + 128, CH):
                on = diagonal_of(r, 128)
                dr = jnp.where(on, mf[0, pl.ds(r, CH), lane] + shift[:, lane], 0.0)
                di = jnp.where(on, mf[1, pl.ds(r, CH), lane] + half[:, lane], 0.0)
                dr_row = dr_row + jnp.sum(dr, 0, keepdims=True)
                di_row = di_row + jnp.sum(di, 0, keepdims=True)
                a, b = jnp.sum(dr, 1, keepdims=True), jnp.sum(di, 1, keepdims=True)
                n = 1.0 / (a * a + b * b)
                cols[r] = (a * n, -b * n)
            n = 1.0 / (dr_row * dr_row + di_row * di_row)
            rows.append((dr_row * n, -di_row * n))
        return tuple(jnp.concatenate([rows[0][c], rows[1][c]], 1) for c in range(2)), cols

    def green_from(i, between):
        (rr, ri), cols = inverse_ends(i)
        for r, _, _ in chunks():
            on = diagonal_of(r, B)
            m_re = jnp.where(on, 0.0, mf[0, pl.ds(r, CH)])
            m_im = jnp.where(on, 0.0, mf[1, pl.ds(r, CH)])
            cr, ci = cols[r]
            a_re = cr * m_re - ci * m_im
            a_im = cr * m_im + ci * m_re
            put_left(al, (), r, CH, a_re, a_im, False)
            mf[0, pl.ds(r, CH)] = jnp.where(on, 1.0, 0.0) - a_re
            mf[1, pl.ds(r, CH)] = -a_im
        sq = dot3(get(al), get(al, both, first))
        between(0)
        for r, a, b in chunks():
            u_re, u_im = sq[a], sq[b]
            put_left(ul, (), r, CH, u_re, u_im, False)
            mf[0, pl.ds(r, CH)] += u_re
            mf[1, pl.ds(r, CH)] += u_im
        cube = dot3(get(ul), get(al, both, first))
        between(1)
        for r, a, b in chunks():
            t_re = mf[0, pl.ds(r, CH)] - cube[a]
            t_im = mf[1, pl.ds(r, CH)] - cube[b]
            g_re = t_re * rr - t_im * ri
            g_im = t_re * ri + t_im * rr
            gf[i, pl.ds(r, CH)] = g_re
            gf[i, pl.ds(B + r, CH)] = g_im
            put(gs, (pl.ds(r, CH),), g_re)
            put(gs, (pl.ds(B + r, CH),), g_im)
            put_left(gl, (), r, CH, g_re, g_im, False)

    def put_source(i, s_re, s_im):
        gamma = source(i)
        for r, a, _ in chunks():
            x = jnp.where(diagonal_of(r, B), gamma, 0.0)
            if s_re is not None:
                x = x + s_re[a]
            put(ss, (pl.ds(r, CH),), x)
            put(ss, (pl.ds(B + r, CH),), jnp.zeros((CH, B), f32) if s_im is None else s_im[a])

    def lesser_left():
        t = dot3(get(gl), get(ss))
        for r, a, b in chunks():
            put_left(tl, (), r, CH, t[a], t[b], True)

    def lesser_of(i):
        w = dot3(get(tl), get(gs))
        for r, a, b in chunks():
            for at, x in ((r, w[a]), (B + r, w[b])):
                wf[i, pl.ds(at, CH)] = x
                put(ws, (pl.ds(at, CH),), x)

    for r, _, _ in chunks():
        mf[0, pl.ds(r, CH)] = -onsite[0, pl.ds(r, CH)]
        mf[1, pl.ds(r, CH)] = jnp.zeros((CH, B), f32)
    put_source(0, None, None)
    green_from(0, lambda stage: None)

    def forward_step(i, carry):
        kind = bk_ref[i - 1]
        v = jnp.where(kind == 0, couplings[0], jnp.where(kind == 1, couplings[1], couplings[2]))
        put(vv, (slice(None),), v)
        put(vt, (slice(None),), v.T)
        p = dot3(get(gs), get(vv))
        for r, a, b in chunks():
            put_left(pr, (i - 1,), r, CH, p[a], p[b], False)
        lesser_left()
        part = lambda j: dot3(get(vt), get(pr, i - 1, pl.ds(j * B, B), first))
        m = part(0), part(1)
        for r, a, _ in chunks():
            mf[0, pl.ds(r, CH)] = -onsite[i, pl.ds(r, CH)] - m[0][a]
            mf[1, pl.ds(r, CH)] = -m[1][a]
        lesser_of(i - 1)

        def between(stage):
            if stage == 0:
                q = dot3(get(ws), get(vv))
                for r, a, b in chunks():
                    put_left(pr, (i - 1,), 2 * B + r, CH, q[a], q[b], True)
            else:
                put_source(i, part(2), part(3))

        green_from(i, between)
        return carry

    lax.fori_loop(1, layers + 1, forward_step, 0)
    pl.semaphore_wait(barrier, len(peers))
    lesser_left()
    lesser_of(layers)
    hf[...] = jnp.zeros_like(hf)

    def report(i, m, r, x):
        if i == layers:
            return
        x = weight * x
        for half in range(0, CH, 16):
            e = (r + half) // 16
            blocks[i, m, e // 4, e // 2 % 2, e % 2] = x[half : half + 16]

    def finish(i, last):
        h_re, h_im = hf[0].T, hf[1].T
        for r, a, _ in chunks():
            w_re = wf[i, pl.ds(r, CH)] + (hf[0, pl.ds(r, CH)] + h_re[a])
            w_im = wf[i, pl.ds(B + r, CH)] + (hf[1, pl.ds(r, CH)] - h_im[a])
            report(i, 0, r, w_re)
            report(i, 1, r, w_im)
            if not last:
                put(ws, (pl.ds(r, CH),), w_re)
                put(ws, (pl.ds(B + r, CH),), w_im)

    def backward(i, inner):
        ends = get(pr, i, first)
        if inner:
            qz = dot3(get(pr, i), get(gs))
            zh = qz[2 * B :]
        else:
            zh = dot3(get(pr, i, pl.ds(2 * B, 2 * B)), get(gs))
        finish(i + 1, False)
        if i < layers - 1:
            core_start(i + 1)
        pw = dot3(get(pr, i, both), get(ws))
        if inner:
            for r, a, b in chunks():
                put_left(al, (), r, CH, qz[a], qz[b], True)
            grown = dot3(get(al), ends, True)
        for r, a, b in chunks():
            cur = pw[a] + zh[a], pw[b] + zh[b]
            report(i, 2, r, cur[0])
            report(i, 3, r, cur[1])
            put_left(ml, (), r, CH, cur[0] - 0.5 * pw[a], cur[1] - 0.5 * pw[b], False)
        if inner:
            for r, a, b in chunks():
                put(gs, (pl.ds(r, CH),), gf[i, pl.ds(r, CH)] + grown[a])
                put(gs, (pl.ds(B + r, CH),), gf[i, pl.ds(B + r, CH)] + grown[b])
        h = dot3(get(ml), ends, True)
        hf[0] = h[0:B]
        hf[1] = h[B:]
        if i == 0:
            plane_turn(3)
        if i < layers - 1:
            core_finish(i + 1)
            plane_start(i + 1)

    backward(3, True)
    for i in (2, 1, 0):
        backward(i, i > 0)
    finish(0, True)
    core_start(0)
    plane_turn(2)
    core_finish(0)
    plane_start(0)
    plane_finish(3)
    line_start(3)
    plane_turn(1)
    plane_finish(2)
    line_start(2)
    plane_turn(0)
    plane_finish(1)
    line_start(1)
    for i in (3, 2, 1):
        line_finish(i)
    plane_finish(0)
    line_start(0)
    line_finish(0)
    owner_exchange()
    for i in range(layers):
        wait(from_core.at[i], core_sems.at[0, i])
        for way in range(2):
            wait(from_first.at[i, way], first_sems.at[0, way, i])
            wait(from_second.at[i, way], second_sems.at[0, way, i])
        wait(from_line.at[i], line_sems.at[0, i])
    wait(at_owner, owner_sems.at[0])


def scratch(layers):
    pair = lambda *s: [pltpu.VMEM(s, bf16), pltpu.VMEM(s, bf16)]
    full = lambda *s: pltpu.VMEM(s, f32)
    wide = pair(2 * B, 2 * B)
    return (
        pair(2 * B, B) + wide + pair(2 * B, B) + pair(layers, 4 * B, 2 * B) + wide + wide
        + pair(2 * B, B) + wide + wide + pair(B, B) + pair(B, B)
        + [full(layers + 1, 2 * B, B)] * 2 + [full(2, B, B)] * 2
        + [
            full(layers, 4, 4, 2, 2, 16, B),
            full(layers, 4, 4, 2, 16, B),
            full(layers, 4, 4, 2, 16, B),
            full(layers, 2, 3, 4, 16, B),
            full(layers, 2, 4, 16, B),
            full(layers, 2, 3, 16, B),
            full(layers, 2, 4, 8, 128),
            full(layers, 7, 8, 128),
            full(layers, 8, 128),
            full(15, 8, 128),
            full(4, 4, 8, 128),
            pltpu.SemaphoreType.DMA((2, layers)),
            pltpu.SemaphoreType.DMA((2, 2, layers)),
            pltpu.SemaphoreType.DMA((2, 2, layers)),
            pltpu.SemaphoreType.DMA((2, layers)),
            pltpu.SemaphoreType.DMA((2,)),
        ]
    )


def per_device(
    energies, momenta, energy_level, momentum_level, energy_table, momentum_table,
    onsite, broad, kdiag, fermi, couplings, bond_kind,
):
    layers = onsite.shape[0] - 1
    args = (
        energies, momenta, energy_level, momentum_level, energy_table, momentum_table,
        fermi, bond_kind, broad, kdiag, couplings, onsite,
    )
    held = [pltpu.VMEM(x.shape, x.dtype) for x in args[8:]]
    owned = pl.pallas_call(
        sweeps,
        out_shape=jax.ShapeDtypeStruct((4, 16, B), f32),
        in_specs=[pl.BlockSpec(memory_space=pltpu.SMEM)] * 8 + [pl.BlockSpec(memory_space=pl.ANY)] * 4,
        out_specs=pl.BlockSpec(memory_space=pltpu.VMEM),
        scratch_shapes=held + [pltpu.SemaphoreType.DMA((4,))] + scratch(layers),
        compiler_params=pltpu.CompilerParams(
            vmem_limit_bytes=62 << 20, collective_id=0, has_side_effects=True
        ),
        name="sweeps",
    )(*args)
    return owned[None, :2], owned[None, 2:]


def solution(mesh):
    rep = P()
    both = P(("energy", "layer"))
    return jax.shard_map(
        per_device,
        mesh=mesh,
        in_specs=(both, P("kpt"), both, P("kpt"), rep, rep, rep, rep, rep, rep, rep, rep),
        out_specs=(P("layer", None, "energy", None), P("layer", None, "energy", None)),
        check_vma=False,
    )
```

time: 82.1 us -> 66.8 us (0.81)
  Pallas kernels: 73.2 us -> 61.9 us
  local copies, waits for them, and re-layouts: 5.34 us -> 1.41 us
    pallas_call x1, Pallas kernels: 73.2 us -> 61.9 us  [per_device(): pl.pallas_call(sweeps, out_shape=jax.ShapeDtypeStruct((4, 16, B), f32), i...]
    unnamed x2 -> x0, local copies, waits for them, and re-layouts: 2.75 us -> none
    broadcast_in_dim x2 -> x1, local copies, waits for them, and re-layouts: 2.59 us -> 1.41 us  [per_device(): return (owned[None, :2], owned[None, 2:])]
where the time goes in v1:
time: 66.8 us; the launch traced here: 66.5 us
  Pallas kernels  61.9 us (93%)
  between operations  3.22 us (5%)
  local copies, waits for them, and re-layouts  1.41 us (2%)
    pallas_call x1, Pallas kernels, per_device(): pl.pallas_call(sweeps, out_shape=jax.ShapeDtypeStruct((4, 16, B), f32), i...  61.9 us
    broadcast_in_dim x1, local copies, waits for them, and re-layouts, per_device(): return (owned[None, :2], owned[None, 2:])  1.41 us

profile of v1, /device:TPU:8, one launch (start us, length us, event | category | flops | bytes accessed | tf_op | source)
XLA Modules:
  0.0 66.5 jit_solution(16785292542482882255)
XLA Ops:
  3.2 61.9 %sweeps.1 = f32[4,16,256]{2,1,0:T(8,128)} custom-call(f32[1]{0:T(128)S(6)} %copy.14.refs_0_, f32[1]{0:T(128)S(6)} %copy.15.refs_1_, s32[1]{0:T(128)S(6)} %copy.16.refs_2_, s32[1]{0:T(128)S(6)} %copy.17.refs_3_, f32[8]{0:T(128)} %refs_4_.1, f32[8]{0:T(128)} %refs_5_.1, f32[5]{0:T(128)} %refs_6_.1, s32[4]{0:T(128)} %refs_7_.1, f32[5,256]{1,0:T(8,128)} %refs_8_.1, ...), custom_call_target="tpu_custom_call" | custom-call | tf_op jit(solution)/shard_map/sweeps/pallas_call | solution.py:444
  65.1 1.4 %slice_bitcast_fusion = (f32[1,2,16,256]{3,2,1,0:T(8,128)}, f32[1,2,16,256]{3,2,1,0:T(8,128)}) fusion(f32[4,16,256]{2,1,0:T(8,128)} %sweeps.1), kind=kLoop, calls=%fused_computation | loop fusion | bytes 131072 | tf_op jit(solution)/shard_map/broadcast_in_dim | solution.py:455

commit v2 on v1

--- a/solution.py
+++ b/solution.py
@@ -36,14 +36,24 @@
     pair[0][at], pair[1][at] = split(x)
 
 
-def put_left(pair, lead, row, rows, re, im, conj):
-    for ref, r, i in zip(pair, split(re), split(im)):
-        top, low = lead + (pl.ds(row, rows),), lead + (pl.ds(row + B, rows),)
-        a, b = pl.ds(0, B), pl.ds(B, B)
-        ref[top + (a,)] = r
-        ref[low + (a,)] = i
-        ref[top + (b,)] = i if conj else -i
-        ref[low + (b,)] = -r if conj else r
+def put3(pair, lead, at, stride, re, im, conj):
+    for n, x in enumerate((re, im, re - im if conj else re + im)):
+        put(pair, lead + (pl.ds(at + n * stride, CH),), x)
+
+
+def product(left, right, conj=False, tb=False):
+    t1, t2, t3 = (dot3(left(n), right(n), tb) for n in range(3))
+
+    def rows(a):
+        if conj:
+            return t1[a] + t2[a], (t1[a] - t2[a]) - t3[a]
+        return t1[a] - t2[a], t3[a] - (t1[a] + t2[a])
+
+    return rows
+
+
+def thirds(pair, *lead):
+    return lambda n: get(pair, *lead, pl.ds(n * B, B))
 
 
 def chunks():
@@ -56,7 +66,10 @@
 ):
     scalars, inputs, result = refs[:8], refs[8:12], refs[12]
     held, in_sems, rest = refs[13:17], refs[17], refs[18:]
-    copies = [pltpu.make_async_copy(a, b, in_sems.at[n]) for n, (a, b) in enumerate(zip(inputs, held))]
+    broad, kdiag, couplings, onsite = zip(inputs, held)
+    first, rest_of = pl.ds(0, 1), pl.ds(1, onsite[0].shape[0] - 1)
+    pairs = [broad, kdiag, [x.at[first] for x in onsite], couplings, [x.at[rest_of] for x in onsite]]
+    copies = [pltpu.make_async_copy(a, b, in_sems.at[n]) for n, (a, b) in enumerate(pairs)]
     for copy in copies:
         copy.start()
     sweep_body(copies, result, *scalars, *held, *rest)
@@ -65,18 +78,16 @@
 def sweep_body(
     copies, result, e_ref, k_ref, el_ref, ml_ref, et_ref, mt_ref, fermi_ref, bk_ref,
     broad, kdiag, couplings, onsite,
-    gs_h, gs_l, gl_h, gl_l, ws_h, ws_l, pr_h, pr_l, al_h, al_l, ul_h, ul_l, ss_h, ss_l,
+    gs_h, gs_l, ws_h, ws_l, pr_h, pr_l, al_h, al_l, ul_h, ul_l, ss_h, ss_l,
     tl_h, tl_l, ml_h, ml_l, v_h, v_l, vt_h, vt_l, gf, wf, mf, hf,
-    blocks, from_core, to_plane, from_first, to_second, from_second, to_line, from_line, to_owner, at_owner, owned,
+    blocks, from_core, to_plane, from_first, to_second, from_second, to_line, from_line, to_owner, many,
     core_sems, first_sems, second_sems, line_sems, owner_sems,
 ):
     layers = onsite.shape[0] - 1
-    gs, gl, ws, pr, al, ul, ss, tl, ml, vv, vt = (
-        (gs_h, gs_l), (gl_h, gl_l), (ws_h, ws_l), (pr_h, pr_l), (al_h, al_l), (ul_h, ul_l),
+    gs, ws, pr, al, ul, ss, tl, ml, vv, vt = (
+        (gs_h, gs_l), (ws_h, ws_l), (pr_h, pr_l), (al_h, al_l), (ul_h, ul_l),
         (ss_h, ss_l), (tl_h, tl_l), (ml_h, ml_l), (v_h, v_l), (vt_h, vt_l),
     )
-    for copy in copies:
-        copy.wait()
     energy = e_ref[0]
     moment = k_ref[0]
     weight = et_ref[el_ref[0]] * mt_ref[ml_ref[0]] * (1.0 / 256)
@@ -179,21 +190,18 @@
         to_owner[i] = total
 
     def owner_exchange():
+        mine = result.at[me_l, lax.div(me_k, 2), :, pl.ds(pl.multiple_of(128 * lax.rem(me_k, 2), 128), 128)]
         for step in range(1, 16):
             k, y = owner_peer(step)
-            send(to_owner.at[y], at_owner.at[step - 1],
-                 (owner_sems.at[0], owner_sems.at[1]), owner_device(step))
-        wait(at_owner, owner_sems.at[1])
-        owned[me_l, me_k] = to_owner[me_l]
-        for step in range(1, 16):
-            k = lax.rem(me_k + 4 - step // 4, 4)
-            y = lax.rem(me_l + 4 - step % 4, 4)
-            owned[y, k] = at_owner[step - 1]
-        for m in range(4):
-            for k in range(4):
-                result[m, pl.ds(8 * (k // 2), 8), pl.ds(128 * (k % 2), 128)] = owned[m, k]
-
-    both, first = pl.ds(0, 2 * B), pl.ds(0, B)
+            send(to_owner.at[y], mine, (owner_sems.at[0], owner_sems.at[1]), owner_device(step))
+        own = pltpu.make_async_copy(to_owner.at[me_l], mine, owner_sems.at[2])
+        own.start()
+        own.wait()
+        wait(many, owner_sems.at[1])
+
+    for copy in copies[:3]:
+        copy.wait()
+    both = pl.ds(0, 2 * B)
 
     def diagonal_of(r, lanes):
         at = r % 128 if lanes == 128 else r
@@ -236,28 +244,27 @@
             cr, ci = cols[r]
             a_re = cr * m_re - ci * m_im
             a_im = cr * m_im + ci * m_re
-            put_left(al, (), r, CH, a_re, a_im, False)
+            put3(al, (), r, B, a_re, a_im, False)
             mf[0, pl.ds(r, CH)] = jnp.where(on, 1.0, 0.0) - a_re
             mf[1, pl.ds(r, CH)] = -a_im
-        sq = dot3(get(al), get(al, both, first))
+        sq = product(thirds(al), thirds(al))
         between(0)
-        for r, a, b in chunks():
-            u_re, u_im = sq[a], sq[b]
-            put_left(ul, (), r, CH, u_re, u_im, False)
+        for r, a, _ in chunks():
+            u_re, u_im = sq(a)
+            put3(ul, (), r, B, u_re, u_im, False)
             mf[0, pl.ds(r, CH)] += u_re
             mf[1, pl.ds(r, CH)] += u_im
-        cube = dot3(get(ul), get(al, both, first))
+        cube = product(thirds(ul), thirds(al))
         between(1)
-        for r, a, b in chunks():
-            t_re = mf[0, pl.ds(r, CH)] - cube[a]
-            t_im = mf[1, pl.ds(r, CH)] - cube[b]
+        for r, a, _ in chunks():
+            c_re, c_im = cube(a)
+            t_re = mf[0, pl.ds(r, CH)] - c_re
+            t_im = mf[1, pl.ds(r, CH)] - c_im
             g_re = t_re * rr - t_im * ri
             g_im = t_re * ri + t_im * rr
             gf[i, pl.ds(r, CH)] = g_re
             gf[i, pl.ds(B + r, CH)] = g_im
-            put(gs, (pl.ds(r, CH),), g_re)
-            put(gs, (pl.ds(B + r, CH),), g_im)
-            put_left(gl, (), r, CH, g_re, g_im, False)
+            put3(gs, (), r, B, g_re, g_im, False)
 
     def put_source(i, s_re, s_im):
         gamma = source(i)
@@ -265,20 +272,21 @@
             x = jnp.where(diagonal_of(r, B), gamma, 0.0)
             if s_re is not None:
                 x = x + s_re[a]
-            put(ss, (pl.ds(r, CH),), x)
-            put(ss, (pl.ds(B + r, CH),), jnp.zeros((CH, B), f32) if s_im is None else s_im[a])
+            put3(ss, (), r, B, x, jnp.zeros((CH, B), f32) if s_im is None else s_im[a], False)
 
     def lesser_left():
-        t = dot3(get(gl), get(ss))
-        for r, a, b in chunks():
-            put_left(tl, (), r, CH, t[a], t[b], True)
+        t = product(thirds(gs), thirds(ss))
+        for r, a, _ in chunks():
+            put3(tl, (), r, B, *t(a), True)
 
     def lesser_of(i):
-        w = dot3(get(tl), get(gs))
-        for r, a, b in chunks():
-            for at, x in ((r, w[a]), (B + r, w[b])):
-                wf[i, pl.ds(at, CH)] = x
-                put(ws, (pl.ds(at, CH),), x)
+        w = product(thirds(tl), thirds(gs), True)
+        for r, a, _ in chunks():
+            w_re, w_im = w(a)
+            wf[i, pl.ds(r, CH)] = w_re
+            wf[i, pl.ds(B + r, CH)] = w_im
+            put(ws, (pl.ds(r, CH),), w_re)
+            put(ws, (pl.ds(B + r, CH),), w_im)
 
     for r, _, _ in chunks():
         mf[0, pl.ds(r, CH)] = -onsite[0, pl.ds(r, CH)]
@@ -291,11 +299,11 @@
         v = jnp.where(kind == 0, couplings[0], jnp.where(kind == 1, couplings[1], couplings[2]))
         put(vv, (slice(None),), v)
         put(vt, (slice(None),), v.T)
-        p = dot3(get(gs), get(vv))
+        p = dot3(get(gs, both), get(vv))
         for r, a, b in chunks():
-            put_left(pr, (i - 1,), r, CH, p[a], p[b], False)
+            put3(pr, (i - 1,), r, 2 * B, p[a], p[b], False)
         lesser_left()
-        part = lambda j: dot3(get(vt), get(pr, i - 1, pl.ds(j * B, B), first))
+        part = lambda j: dot3(get(vt), get(pr, i - 1, pl.ds((0, 2, 1, 3)[j] * B, B)))
         m = part(0), part(1)
         for r, a, _ in chunks():
             mf[0, pl.ds(r, CH)] = -onsite[i, pl.ds(r, CH)] - m[0][a]
@@ -304,15 +312,17 @@
 
         def between(stage):
             if stage == 0:
-                q = dot3(get(ws), get(vv))
+                q = dot3(get(ws, both), get(vv))
                 for r, a, b in chunks():
-                    put_left(pr, (i - 1,), 2 * B + r, CH, q[a], q[b], True)
+                    put3(pr, (i - 1,), B + r, 2 * B, q[a], q[b], True)
             else:
                 put_source(i, part(2), part(3))
 
         green_from(i, between)
         return carry
 
+    for copy in copies[3:]:
+        copy.wait()
     lax.fori_loop(1, layers + 1, forward_step, 0)
     pl.semaphore_wait(barrier, len(peers))
     lesser_left()
@@ -335,36 +345,34 @@
             report(i, 0, r, w_re)
             report(i, 1, r, w_im)
             if not last:
-                put(ws, (pl.ds(r, CH),), w_re)
-                put(ws, (pl.ds(B + r, CH),), w_im)
+                put3(ws, (), r, B, w_re, w_im, False)
 
     def backward(i, inner):
-        ends = get(pr, i, first)
+        from_left = lambda n: get(pr, i, pl.ds(2 * n * B, B))
+        from_right = lambda n: get(pr, i, pl.ds((2 * n + 1) * B, B))
         if inner:
-            qz = dot3(get(pr, i), get(gs))
-            zh = qz[2 * B :]
-        else:
-            zh = dot3(get(pr, i, pl.ds(2 * B, 2 * B)), get(gs))
+            q = product(from_left, thirds(gs))
+        z = product(from_right, thirds(gs), True)
         finish(i + 1, False)
         if i < layers - 1:
             core_start(i + 1)
-        pw = dot3(get(pr, i, both), get(ws))
+        pw = product(from_left, thirds(ws))
         if inner:
-            for r, a, b in chunks():
-                put_left(al, (), r, CH, qz[a], qz[b], True)
-            grown = dot3(get(al), ends, True)
-        for r, a, b in chunks():
-            cur = pw[a] + zh[a], pw[b] + zh[b]
-            report(i, 2, r, cur[0])
-            report(i, 3, r, cur[1])
-            put_left(ml, (), r, CH, cur[0] - 0.5 * pw[a], cur[1] - 0.5 * pw[b], False)
+            for r, a, _ in chunks():
+                put3(al, (), r, B, *q(a), False)
+            grown = product(thirds(al), from_left, False, True)
+        for r, a, _ in chunks():
+            (p_re, p_im), (z_re, z_im) = pw(a), z(a)
+            report(i, 2, r, p_re + z_re)
+            report(i, 3, r, p_im + z_im)
+            put3(ml, (), r, B, 0.5 * p_re + z_re, 0.5 * p_im + z_im, True)
         if inner:
-            for r, a, b in chunks():
-                put(gs, (pl.ds(r, CH),), gf[i, pl.ds(r, CH)] + grown[a])
-                put(gs, (pl.ds(B + r, CH),), gf[i, pl.ds(B + r, CH)] + grown[b])
-        h = dot3(get(ml), ends, True)
-        hf[0] = h[0:B]
-        hf[1] = h[B:]
+            for r, a, _ in chunks():
+                n_re, n_im = grown(a)
+                put3(gs, (), r, B, gf[i, pl.ds(r, CH)] + n_re, gf[i, pl.ds(B + r, CH)] + n_im, False)
+        h = product(thirds(ml), from_left, True, True)
+        for r, a, _ in chunks():
+            hf[0, pl.ds(r, CH)], hf[1, pl.ds(r, CH)] = h(a)
         if i == 0:
             plane_turn(3)
         if i < layers - 1:
@@ -399,16 +407,16 @@
             wait(from_first.at[i, way], first_sems.at[0, way, i])
             wait(from_second.at[i, way], second_sems.at[0, way, i])
         wait(from_line.at[i], line_sems.at[0, i])
-    wait(at_owner, owner_sems.at[0])
+    wait(many, owner_sems.at[0])
 
 
 def scratch(layers):
     pair = lambda *s: [pltpu.VMEM(s, bf16), pltpu.VMEM(s, bf16)]
     full = lambda *s: pltpu.VMEM(s, f32)
-    wide = pair(2 * B, 2 * B)
+    three = pair(3 * B, B)
     return (
-        pair(2 * B, B) + wide + pair(2 * B, B) + pair(layers, 4 * B, 2 * B) + wide + wide
-        + pair(2 * B, B) + wide + wide + pair(B, B) + pair(B, B)
+        three + three + pair(layers, 6 * B, B) + three + three + three + three + three
+        + pair(B, B) + pair(B, B)
         + [full(layers + 1, 2 * B, B)] * 2 + [full(2, B, B)] * 2
         + [
             full(layers, 4, 4, 2, 2, 16, B),
@@ -421,12 +429,11 @@
             full(layers, 7, 8, 128),
             full(layers, 8, 128),
             full(15, 8, 128),
-            full(4, 4, 8, 128),
             pltpu.SemaphoreType.DMA((2, layers)),
             pltpu.SemaphoreType.DMA((2, 2, layers)),
             pltpu.SemaphoreType.DMA((2, 2, layers)),
             pltpu.SemaphoreType.DMA((2, layers)),
-            pltpu.SemaphoreType.DMA((2,)),
+            pltpu.SemaphoreType.DMA((3,)),
         ]
     )
 
@@ -443,15 +450,15 @@
     held = [pltpu.VMEM(x.shape, x.dtype) for x in args[8:]]
     owned = pl.pallas_call(
         sweeps,
-        out_shape=jax.ShapeDtypeStruct((4, 16, B), f32),
+        out_shape=jax.ShapeDtypeStruct((4, 2, 8, B), f32),
         in_specs=[pl.BlockSpec(memory_space=pltpu.SMEM)] * 8 + [pl.BlockSpec(memory_space=pl.ANY)] * 4,
-        out_specs=pl.BlockSpec(memory_space=pltpu.VMEM),
-        scratch_shapes=held + [pltpu.SemaphoreType.DMA((4,))] + scratch(layers),
+        out_specs=pl.BlockSpec(memory_space=pl.ANY),
+        scratch_shapes=held + [pltpu.SemaphoreType.DMA((5,))] + scratch(layers),
         compiler_params=pltpu.CompilerParams(
             vmem_limit_bytes=62 << 20, collective_id=0, has_side_effects=True
         ),
         name="sweeps",
-    )(*args)
+    )(*args).reshape(4, 16, B)
     return owned[None, :2], owned[None, 2:]
 
 

time: 66.8 us -> 60.9 us (0.912)
  Pallas kernels: 61.9 us -> 56.1 us
    pallas_call x1, Pallas kernels: 61.9 us -> 56.1 us  [per_device(): pl.pallas_call(sweeps, out_shape=jax.ShapeDtypeStruct((4, 2, 8, B), f32),...]
where the time goes in v2:
time: 60.9 us; the launch traced here: 60.7 us
  Pallas kernels  56.1 us (92%)
  between operations  3.22 us (5%)
  local copies, waits for them, and re-layouts  1.41 us (2%)
    pallas_call x1, Pallas kernels, per_device(): pl.pallas_call(sweeps, out_shape=jax.ShapeDtypeStruct((4, 2, 8, B), f32),...  56.1 us
    broadcast_in_dim x1, local copies, waits for them, and re-layouts, per_device(): return (owned[None, :2], owned[None, 2:])  1.41 us

profile of v2, /device:TPU:8, one launch (start us, length us, event | category | flops | bytes accessed | tf_op | source)
XLA Modules:
  0.0 60.7 jit_solution(12116829318536861196)
XLA Ops:
  3.2 56.1 %sweeps.1 = f32[4,2,8,256]{3,2,1,0:T(8,128)} custom-call(f32[1]{0:T(128)S(6)} %copy.14.refs_0_, f32[1]{0:T(128)S(6)} %copy.15.refs_1_, s32[1]{0:T(128)S(6)} %copy.16.refs_2_, s32[1]{0:T(128)S(6)} %copy.17.refs_3_, f32[8]{0:T(128)} %refs_4_.1, f32[8]{0:T(128)} %refs_5_.1, f32[5]{0:T(128)} %refs_6_.1, s32[4]{0:T(128)} %refs_7_.1, f32[5,256]{1,0:T(8,128)} %refs_8_.1, ...), custom_call_target="tpu_custom_call" | custom-call | tf_op jit(solution)/shard_map/sweeps/pallas_call | solution.py:451
  59.3 1.4 %slice_bitcast_fusion = (f32[1,2,16,256]{3,2,1,0:T(8,128)}, f32[1,2,16,256]{3,2,1,0:T(8,128)}) fusion(f32[4,2,8,256]{3,2,1,0:T(8,128)} %sweeps.1), kind=kLoop, calls=%fused_computation | loop fusion | bytes 131072 | tf_op jit(solution)/shard_map/broadcast_in_dim | solution.py:462

commit v3 on v2

--- a/solution.py
+++ b/solution.py
@@ -80,7 +80,7 @@
     broad, kdiag, couplings, onsite,
     gs_h, gs_l, ws_h, ws_l, pr_h, pr_l, al_h, al_l, ul_h, ul_l, ss_h, ss_l,
     tl_h, tl_l, ml_h, ml_l, v_h, v_l, vt_h, vt_l, gf, wf, mf, hf,
-    blocks, from_core, to_plane, from_first, to_second, from_second, to_line, from_line, to_owner, many,
+    blocks, from_core, rows_x, tiles_y, from_x, from_y, second, from_second, to_line, from_line, to_owner, many,
     core_sems, first_sems, second_sems, line_sems, owner_sems,
 ):
     layers = onsite.shape[0] - 1
@@ -144,53 +144,67 @@
 
     def core_finish(i):
         wait(from_core.at[i], core_sems.at[1, i])
-        to_plane[i] = blocks[i, :, :, :, me_c] + from_core[i]
+        for m in range(4):
+            for x in range(4):
+                rows_x[i, m, x] = blocks[i, m, x, 0, me_c] + from_core[i, m, x, 0]
+                other = blocks[i, m, x, 1, me_c] + from_core[i, m, x, 1]
+                for k in range(4):
+                    row, col = 8 * (k // 2), 128 * (k % 2)
+                    tiles_y[i, m, x, k] = other[row : row + 8, col : col + 128]
 
     def plane_start(i):
         for step in range(1, 4):
-            send(to_plane.at[i, :, after(me_x, step), 0], from_first.at[i, 0, step - 1],
+            send(rows_x.at[i, :, after(me_x, step)], from_x.at[i, step - 1],
                  (first_sems.at[0, 0, i], first_sems.at[1, 0, i]), x_device(step))
-            send(to_plane.at[i, after(me_l, step), :, 1], from_first.at[i, 1, step - 1],
+            send(tiles_y.at[i, :, :, after(me_l, step)], from_y.at[i, step - 1],
                  (first_sems.at[0, 1, i], first_sems.at[1, 1, i]), y_device(step))
 
-    def plane_turn(i):
-        for way in range(2):
-            wait(from_first.at[i, way], first_sems.at[1, way, i])
-            own = to_plane[i, :, me_x, 0] if way == 0 else to_plane[i, me_l, :, 1]
-            to_second[i, way] = own + from_first[i, way, 0] + (
-                from_first[i, way, 1] + from_first[i, way, 2]
-            )
-        for step in range(1, 4):
-            send(to_second.at[i, 0, after(me_l, step)], from_second.at[i, 0, step - 1],
-                 (second_sems.at[0, 0, i], second_sems.at[1, 0, i]), y_device(step))
-            send(to_second.at[i, 1, after(me_x, step)], from_second.at[i, 1, step - 1],
-                 (second_sems.at[0, 1, i], second_sems.at[1, 1, i]), x_device(step))
-
-    def plane_finish(i):
-        for z in range(2):
-            wait(from_second.at[i, z], second_sems.at[1, z, i])
-            total = to_second[i, z, me_l if z == 0 else me_x] + from_second[i, z, 0] + (
-                from_second[i, z, 1] + from_second[i, z, 2]
-            )
+    def plane_gather(i):
+        wait(from_x.at[i], first_sems.at[1, 0, i])
+        for m in range(4):
+            total = rows_x[i, m, me_x] + from_x[i, 0, m] + (from_x[i, 1, m] + from_x[i, 2, m])
             for k in range(4):
                 row, col = 8 * (k // 2), 128 * (k % 2)
-                to_line[i, z, k] = total[row : row + 8, col : col + 128]
-
-    def line_start(i):
+                second[i, 0, m, k] = total[row : row + 8, col : col + 128]
+        wait(from_y.at[i], first_sems.at[1, 1, i])
+        for m in range(4):
+            second[i, 1, m] = tiles_y[i, m, :, me_l] + from_y[i, 0, m] + (
+                from_y[i, 1, m] + from_y[i, 2, m]
+            )
+
+    def plane_turn(lo, n):
+        some = pl.ds(lo, n)
+        for step in range(1, 4):
+            send(second.at[some, 0, :, after(me_l, step)], from_second.at[some, 0, step - 1],
+                 (second_sems.at[0, 0, lo], second_sems.at[1, 0, lo]), y_device(step))
+            send(second.at[some, 1, :, after(me_x, step)], from_second.at[some, 1, step - 1],
+                 (second_sems.at[0, 1, lo], second_sems.at[1, 1, lo]), x_device(step))
+
+    def line_start(lo, n):
+        some = pl.ds(lo, n)
+        for z in range(2):
+            wait(from_second.at[some, z], second_sems.at[1, z, lo])
+            for i in range(lo, lo + n):
+                for m in range(4):
+                    own = second[i, z, m, me_l if z == 0 else me_x]
+                    to_line[i, z, m] = own + from_second[i, z, 0, m] + (
+                        from_second[i, z, 1, m] + from_second[i, z, 2, m]
+                    )
         for step in range(1, 8):
             z, k = line_peer(step)
-            send(to_line.at[i, z, k], from_line.at[i, step - 1],
-                 (line_sems.at[0, i], line_sems.at[1, i]), line_device(step))
-
-    def line_finish(i):
-        wait(from_line.at[i], line_sems.at[1, i])
-        total = to_line[i, me_z, me_k]
-        for step in range(1, 8):
-            total = total + from_line[i, step - 1]
-        to_owner[i] = total
+            send(to_line.at[some, z, k], from_line.at[some, step - 1],
+                 (line_sems.at[0, lo], line_sems.at[1, lo]), line_device(step))
+
+    def line_finish(lo, n):
+        wait(from_line.at[pl.ds(lo, n)], line_sems.at[1, lo])
+        for i in range(lo, lo + n):
+            total = to_line[i, me_z, me_k]
+            for step in range(1, 8):
+                total = total + from_line[i, step - 1]
+            to_owner[i] = total
 
     def owner_exchange():
-        mine = result.at[me_l, lax.div(me_k, 2), :, pl.ds(pl.multiple_of(128 * lax.rem(me_k, 2), 128), 128)]
+        mine = result.at[me_k, lax.div(me_l, 2), :, pl.ds(pl.multiple_of(128 * lax.rem(me_l, 2), 128), 128)]
         for step in range(1, 16):
             k, y = owner_peer(step)
             send(to_owner.at[y], mine, (owner_sems.at[0], owner_sems.at[1]), owner_device(step))
@@ -373,8 +387,6 @@
         h = product(thirds(ml), from_left, True, True)
         for r, a, _ in chunks():
             hf[0, pl.ds(r, CH)], hf[1, pl.ds(r, CH)] = h(a)
-        if i == 0:
-            plane_turn(3)
         if i < layers - 1:
             core_finish(i + 1)
             plane_start(i + 1)
@@ -384,29 +396,28 @@
         backward(i, i > 0)
     finish(0, True)
     core_start(0)
-    plane_turn(2)
+    plane_gather(3)
+    plane_gather(2)
     core_finish(0)
     plane_start(0)
-    plane_finish(3)
-    line_start(3)
-    plane_turn(1)
-    plane_finish(2)
-    line_start(2)
-    plane_turn(0)
-    plane_finish(1)
-    line_start(1)
-    for i in (3, 2, 1):
-        line_finish(i)
-    plane_finish(0)
-    line_start(0)
-    line_finish(0)
+    plane_gather(1)
+    plane_turn(1, 3)
+    plane_gather(0)
+    plane_turn(0, 1)
+    line_start(1, 3)
+    line_start(0, 1)
+    line_finish(1, 3)
+    line_finish(0, 1)
     owner_exchange()
     for i in range(layers):
         wait(from_core.at[i], core_sems.at[0, i])
+        wait(from_x.at[i], first_sems.at[0, 0, i])
+        wait(from_y.at[i], first_sems.at[0, 1, i])
+    for lo, n in ((0, 1), (1, 3)):
+        some = pl.ds(lo, n)
         for way in range(2):
-            wait(from_first.at[i, way], first_sems.at[0, way, i])
-            wait(from_second.at[i, way], second_sems.at[0, way, i])
-        wait(from_line.at[i], line_sems.at[0, i])
+            wait(from_second.at[some, way], second_sems.at[0, way, lo])
+        wait(from_line.at[some], line_sems.at[0, lo])
     wait(many, owner_sems.at[0])
 
 
@@ -421,18 +432,20 @@
         + [
             full(layers, 4, 4, 2, 2, 16, B),
             full(layers, 4, 4, 2, 16, B),
-            full(layers, 4, 4, 2, 16, B),
-            full(layers, 2, 3, 4, 16, B),
-            full(layers, 2, 4, 16, B),
-            full(layers, 2, 3, 16, B),
+            full(layers, 4, 4, 16, B),
+            full(layers, 4, 4, 4, 8, 128),
+            full(layers, 3, 4, 16, B),
+            full(layers, 3, 4, 4, 8, 128),
+            full(layers, 2, 4, 4, 8, 128),
+            full(layers, 2, 3, 4, 8, 128),
             full(layers, 2, 4, 8, 128),
             full(layers, 7, 8, 128),
             full(layers, 8, 128),
             full(15, 8, 128),
             pltpu.SemaphoreType.DMA((2, layers)),
             pltpu.SemaphoreType.DMA((2, 2, layers)),
-            pltpu.SemaphoreType.DMA((2, 2, layers)),
-            pltpu.SemaphoreType.DMA((2, layers)),
+            pltpu.SemaphoreType.DMA((2, 2, 2)),
+            pltpu.SemaphoreType.DMA((2, 2)),
             pltpu.SemaphoreType.DMA((3,)),
         ]
     )

time: 60.9 us -> 57 us (0.936)
  Pallas kernels: 56.1 us -> 52.2 us
    pallas_call x1, Pallas kernels: 56.1 us -> 52.2 us  [per_device(): pl.pallas_call(sweeps, out_shape=jax.ShapeDtypeStruct((4, 2, 8, B), f32),...]
where the time goes in v3:
time: 57 us; the launch traced here: 56.8 us
  Pallas kernels  52.2 us (92%)
  between operations  3.22 us (6%)
  local copies, waits for them, and re-layouts  1.41 us (2%)
    pallas_call x1, Pallas kernels, per_device(): pl.pallas_call(sweeps, out_shape=jax.ShapeDtypeStruct((4, 2, 8, B), f32),...  52.2 us
    broadcast_in_dim x1, local copies, waits for them, and re-layouts, per_device(): return (owned[None, :2], owned[None, 2:])  1.41 us

profile of v3, /device:TPU:8, one launch (start us, length us, event | category | flops | bytes accessed | tf_op | source)
XLA Modules:
  0.0 56.8 jit_solution(592257434783587877)
XLA Ops:
  3.2 52.2 %sweeps.1 = f32[4,2,8,256]{3,2,1,0:T(8,128)} custom-call(f32[1]{0:T(128)S(6)} %copy.14.refs_0_, f32[1]{0:T(128)S(6)} %copy.15.refs_1_, s32[1]{0:T(128)S(6)} %copy.16.refs_2_, s32[1]{0:T(128)S(6)} %copy.17.refs_3_, f32[8]{0:T(128)} %refs_4_.1, f32[8]{0:T(128)} %refs_5_.1, f32[5]{0:T(128)} %refs_6_.1, s32[4]{0:T(128)} %refs_7_.1, f32[5,256]{1,0:T(8,128)} %refs_8_.1, ...), custom_call_target="tpu_custom_call" | custom-call | tf_op jit(solution)/shard_map/sweeps/pallas_call | solution.py:464
  55.4 1.4 %slice_bitcast_fusion = (f32[1,2,16,256]{3,2,1,0:T(8,128)}, f32[1,2,16,256]{3,2,1,0:T(8,128)}) fusion(f32[4,2,8,256]{3,2,1,0:T(8,128)} %sweeps.1), kind=kLoop, calls=%fused_computation | loop fusion | bytes 131072 | tf_op jit(solution)/shard_map/broadcast_in_dim | solution.py:475

commit v4 on v3

--- a/solution.py
+++ b/solution.py
@@ -203,11 +203,30 @@
                 total = total + from_line[i, step - 1]
             to_owner[i] = total
 
-    def owner_exchange():
-        mine = result.at[me_k, lax.div(me_l, 2), :, pl.ds(pl.multiple_of(128 * lax.rem(me_l, 2), 128), 128)]
+    mine = result.at[
+        me_k, lax.div(me_l, 2), :, pl.ds(pl.multiple_of(128 * lax.rem(me_l, 2), 128), 128)
+    ]
+
+    def owner_send(k, y):
+        send(to_owner.at[y], mine, (owner_sems.at[0], owner_sems.at[1]),
+             device(me_x, me_z, me_c, k, y))
+
+    def owners_above():
         for step in range(1, 16):
             k, y = owner_peer(step)
-            send(to_owner.at[y], mine, (owner_sems.at[0], owner_sems.at[1]), owner_device(step))
+
+            @pl.when(y != 0)
+            def _():
+                owner_send(k, y)
+
+    def owner_exchange():
+        for step in range(1, 4):
+            owner_send(after(me_k, step), 0)
+
+        @pl.when(me_l != 0)
+        def _():
+            owner_send(me_k, 0)
+
         own = pltpu.make_async_copy(to_owner.at[me_l], mine, owner_sems.at[2])
         own.start()
         own.wait()
@@ -397,9 +416,9 @@
     finish(0, True)
     core_start(0)
     plane_gather(3)
-    plane_gather(2)
     core_finish(0)
     plane_start(0)
+    plane_gather(2)
     plane_gather(1)
     plane_turn(1, 3)
     plane_gather(0)
@@ -407,6 +426,7 @@
     line_start(1, 3)
     line_start(0, 1)
     line_finish(1, 3)
+    owners_above()
     line_finish(0, 1)
     owner_exchange()
     for i in range(layers):

time: 57 us -> 56.2 us (0.986); the launches traced: 56.8 us -> 55.3 us
  Pallas kernels: 52.2 us -> 50.7 us
    pallas_call x1, Pallas kernels: 52.2 us -> 50.7 us  [per_device(): pl.pallas_call(sweeps, out_shape=jax.ShapeDtypeStruct((4, 2, 8, B), f32),...]
where the time goes in v4:
time: 56.2 us; the launch traced here: 55.3 us
  Pallas kernels  50.7 us (90%)
  between operations  3.22 us (6%)
  local copies, waits for them, and re-layouts  1.41 us (3%)
    pallas_call x1, Pallas kernels, per_device(): pl.pallas_call(sweeps, out_shape=jax.ShapeDtypeStruct((4, 2, 8, B), f32),...  50.7 us
    broadcast_in_dim x1, local copies, waits for them, and re-layouts, per_device(): return (owned[None, :2], owned[None, 2:])  1.41 us

profile of v4, /device:TPU:8, one launch (start us, length us, event | category | flops | bytes accessed | tf_op | source)
XLA Modules:
  0.0 55.3 jit_solution(18319416790773658177)
XLA Ops:
  3.2 50.7 %sweeps.1 = f32[4,2,8,256]{3,2,1,0:T(8,128)} custom-call(f32[1]{0:T(128)S(6)} %copy.14.refs_0_, f32[1]{0:T(128)S(6)} %copy.15.refs_1_, s32[1]{0:T(128)S(6)} %copy.16.refs_2_, s32[1]{0:T(128)S(6)} %copy.17.refs_3_, f32[8]{0:T(128)} %refs_4_.1, f32[8]{0:T(128)} %refs_5_.1, f32[5]{0:T(128)} %refs_6_.1, s32[4]{0:T(128)} %refs_7_.1, f32[5,256]{1,0:T(8,128)} %refs_8_.1, ...), custom_call_target="tpu_custom_call" | custom-call | tf_op jit(solution)/shard_map/sweeps/pallas_call | solution.py:484
  53.9 1.4 %slice_bitcast_fusion = (f32[1,2,16,256]{3,2,1,0:T(8,128)}, f32[1,2,16,256]{3,2,1,0:T(8,128)}) fusion(f32[4,2,8,256]{3,2,1,0:T(8,128)} %sweeps.1), kind=kLoop, calls=%fused_computation | loop fusion | bytes 131072 | tf_op jit(solution)/shard_map/broadcast_in_dim | solution.py:495
